TPU v7x, 128 devices: a whole 4x4x4 slice. The times are simulated.
128 devices in a mesh: blk: 64 (over x_lo, y, z, core), tensor: 2 (over x_hi).
Axes of the slice: x: 4 (x_hi: 2, x_lo: 2; x = x_hi * 2 + x_lo), y: 4, z: 4, core: 2. Of those that a mesh axis runs over, the one named last changes fastest.
Arguments:
- tokens: bfloat16 [256, 8192], P('blk'), may hold values from -6 to 6
- gate_weight: bfloat16 [29568, 8192], P(('blk', 'tensor')), may hold values from -0.0625 to 0.0625
- up_weight: bfloat16 [29568, 8192], P(('blk', 'tensor')), may hold values from -0.0625 to 0.0625
- down_weight: bfloat16 [29568, 8192], P(('blk', 'tensor')), may hold values from -0.03125 to 0.03125
Outputs:
- mixed: bfloat16 [256, 8192], P(('blk', 'tensor'))
All inputs are finite; a program needn't handle non-finite values.
Results may differ from a plain program's by a relative error of at most 0.009.
Values may be sent and summed in bfloat16 or wider, within the bound.
No kernel may reach another device: no remote copies, remote signals or barrier semaphores. Data moves between devices by JAX's collectives and lax.ppermute only.
A program may use at most 64 MiB of HBM per device.

v0:
```python
import functools

import jax
import jax.numpy as jnp
from jax import lax
from jax.experimental import pallas as pl
from jax.experimental.pallas import tpu as pltpu
from jax.sharding import PartitionSpec as P


ALL = ("blk", "tensor")
BF = jnp.bfloat16
F32 = jnp.float32
R4 = range(4)


def flat(x, y, z, c):
    return ((x % 2 * 4 + y) * 4 + z) * 4 + c * 2 + x // 2


def move(v, to):
    pairs = [
        (flat(x, y, z, c), flat(*to(x, y, z, c)))
        for x in R4
        for y in R4
        for z in R4
        for c in range(2)
    ]
    return lax.ppermute(v, ALL, pairs)


def core(v):
    return move(v, lambda x, y, z, c: (x, y, z, 1 - c))


def ring(v, k):
    return move(
        v,
        lambda x, y, z, c: (x, (y + k) % 4, z, c) if c else (x, y, (z + k) % 4, c),
    )


def side(v, k):
    return move(
        v,
        lambda x, y, z, c: (x, y, (z + k) % 4, c) if c else (x, (y + k) % 4, z, c),
    )


def first_pair(v):
    here = ring(v, 2)
    there = move(
        v,
        lambda x, y, z, c: (
            (x ^ 1, (y + 2) % 4, z, c) if c else (x ^ 1, y, (z + 2) % 4, c)
        ),
    )
    return here, there


def plane_groups():
    return [
        [
            flat(h * 2 + l, m if c == 0 else s, s if c == 0 else m, c)
            for l in range(2)
            for m in R4
            for h in range(2)
        ]
        for c in range(2)
        for s in R4
    ]


def rows_of(left, weight):
    return lax.dot_general(
        left, weight, (((1,), (1,)), ((), ())), preferred_element_type=F32
    )


def hidden_of(x_refs, gate_ref, up_ref):
    d = x_refs[0].shape[2]
    x = jnp.concatenate([r[...].reshape(-1, d) for r in x_refs], axis=0)
    gate = rows_of(gate_ref[...], x)
    up = rows_of(up_ref[...], x)
    return (gate / (1.0 + jnp.exp(-gate)) * up).T.astype(BF)


def hidden_kernel(*refs):
    *x_refs, gate_ref, up_ref, hidden_ref = refs
    hidden_ref[...] = hidden_of(x_refs, gate_ref, up_ref)


def work_kernel(*refs):
    *x_refs, gate_ref, up_ref, down_ref, sib_ref, own_ref = refs
    down_rows(hidden_of(x_refs, gate_ref, up_ref), down_ref, sib_ref, own_ref)


def down_kernel(hidden_ref, *refs):
    down_rows(hidden_ref[...], *refs)


def down_rows(hidden, down_ref, sib_ref, own_ref):
    part = jnp.dot(hidden, down_ref[...], preferred_element_type=F32)
    rows = own_ref.shape[0]
    own_ref[...] = part[:rows]
    sib_ref[...] = part[rows:].astype(BF).reshape(sib_ref.shape)


def add_kernel(own_ref, fold_ref, *outs):
    d = own_ref.shape[1]
    part = own_ref[...] + fold_ref[...].reshape(-1, d).astype(F32)
    each = part.shape[0] // len(outs)
    for i, o in enumerate(outs):
        o[...] = part[i * each : (i + 1) * each].astype(BF).reshape(o.shape)


def ring_kernel(which, own_ref, fold_ref, lent_ref, out_ref):
    n = out_ref.shape[0]
    d = own_ref.shape[1]
    part = own_ref[2 * n * which : 2 * n * (which + 1), :]
    part += fold_ref[n * which : n * (which + 1)].reshape(-1, d).astype(F32)
    lent = part[n * which : n * (which + 1)] + lent_ref[...].reshape(n, d).astype(F32)
    kept = part[n * (1 - which) : n * (2 - which)]
    h = n // 2
    out_ref[h * which : h * (which + 1)] = lent.astype(BF).reshape(h, 2, d)
    out_ref[h * (1 - which) : h * (2 - which)] = kept.astype(BF).reshape(h, 2, d)


VM = pl.BlockSpec(memory_space=pltpu.VMEM)


def call(kernel, shapes, *args):
    return pl.pallas_call(
        kernel,
        out_shape=shapes,
        in_specs=[VM] * len(args),
        out_specs=[VM] * len(shapes),
        compiler_params=pltpu.CompilerParams(vmem_limit_bytes=12 * 2**20),
    )(*args)


def piece(blocks, d):
    return jax.ShapeDtypeStruct((blocks, 2, d), BF)


def work(weights, *xs):
    d = xs[0].shape[2]
    rows = sum(x.shape[0] * x.shape[1] for x in xs) // 2
    shapes = [piece(rows // 2, d), jax.ShapeDtypeStruct((rows, d), F32)]
    return call(work_kernel, shapes, *xs, *weights)


def add(outs, own, *pieces):
    return call(add_kernel, outs, own, *pieces)


def place_kernel(own_ref, fold_ref, low_ref, high_ref, out_ref):
    me = lax.axis_index("blk")
    own_m = lax.select(me % 2 == 0, me // 8 % 4, me // 2 % 4)
    d = own_ref.shape[1]
    part = own_ref[...]
    for r in (fold_ref, low_ref, high_ref):
        part += r[...].reshape(-1, d).astype(F32)
    for i in range(8):
        m = (own_m + (0, 3, 1, 2)[i // 2]) % 4
        xl = (me // 32 + i % 2) % 2
        out_ref[pl.ds((xl * 4 + m) * 2, 2)] = (
            part[4 * i : 4 * i + 4].astype(BF).reshape(2, 2, d)
        )


def touch_kernel(*refs):
    *weights, out = refs
    out[...] = sum(w[0:8, 0:128].astype(F32) for w in weights)


def touch(*weights):
    return pl.pallas_call(
        touch_kernel,
        out_shape=jax.ShapeDtypeStruct((8, 128), F32),
        in_specs=[VM] * len(weights),
        out_specs=VM,
        compiler_params=pltpu.CompilerParams(
            vmem_limit_bytes=12 * 2**20, has_side_effects=True
        ),
    )(*weights)


def per_device(tokens, gate_weight, up_weight, down_weight):
    rows, d = tokens.shape
    here, there = first_pair(tokens)
    touch(gate_weight)
    touch(up_weight)
    near = jnp.stack([here, there])
    below = side(near, 1)
    above = side(near, -1)
    across = side(near, 2)
    two = jnp.concatenate([near, below, above, across])
    two_sib = core(two)
    low = ring(two, 1)
    high = ring(two, -1)
    weights = (gate_weight, up_weight, down_weight)
    shape = jax.ShapeDtypeStruct((16 * rows, gate_weight.shape[0]), BF)
    (hidden,) = call(hidden_kernel, [shape], two, two_sib, *weights[:2])
    shapes = [piece(16, d), jax.ShapeDtypeStruct((8 * rows, d), F32)]
    part, own_part = call(down_kernel, shapes, hidden, down_weight)
    part = core(part)
    part_a, part_b = add([piece(8, d)] * 2, own_part, part)
    lent_low = ring(part_a, 1)
    lent_high = ring(part_b, -1)

    low_sib = core(low)
    high_sib = core(high)
    own_a = ring(low[:4], 1)
    own_b = ring(high[4:], -1)
    part, own_part = work(weights, low, high, low_sib, high_sib)
    part = core(part)
    (part_low,) = call(
        functools.partial(ring_kernel, 0), [piece(16, d)], own_part, part, lent_low
    )
    back_low = ring(part_low, 1)
    (part_high,) = call(
        functools.partial(ring_kernel, 1), [piece(16, d)], own_part, part, lent_high
    )
    back_high = ring(part_high, -1)

    sib_a = core(own_a)
    sib_b = core(own_b)
    part, own_part = work(weights, own_a, own_b, sib_a, sib_b)
    part = core(part)
    (part,) = call(place_kernel, [piece(16, d)], own_part, part, back_low, back_high)
    pieces = lax.all_to_all(
        part, ALL, 0, 0, axis_index_groups=plane_groups(), tiled=True
    )
    return jnp.sum(pieces.astype(F32), axis=0).astype(BF)


def solution(mesh):
    return jax.shard_map(
        per_device,
        mesh=mesh,
        in_specs=(P("blk", None), P(ALL, None), P(ALL, None), P(ALL, None)),
        out_specs=P(ALL, None),
        check_vma=False,
    )
```

profile of v0, /device:TPU:0, one launch (start us, length us, event | category | flops | bytes accessed | tf_op | source)
XLA Modules:
  0.0 95.0 jit_solution(8964651955827600819)
XLA Ops:
  0.0 4.0 %collective-permute-start = (bf16[4,8192]{1,0:T(4,128)(2,1)}, bf16[4,8192]{1,0:T(4,128)(2,1)S(1)}, u32[]{:S(2)}, u32[]{:S(2)}) collective-permute-start(bf16[4,8192]{1,0:T(4,128)(2,1)} %param.4), channel_id=1, source_target_pairs={{0,8},{2,34},{4,12},{6,38},{8,0},{10,42},{12,4},{14,46},{16,24},{1... | collective-permute-start | bytes 196616 | tf_op jit(solution)/shard_map/ppermute | solution.py:29
  4.0 0.9 collective-permute-start.1
  4.9 1.5 %collective-permute-done = bf16[4,8192]{1,0:T(4,128)(2,1)S(1)} collective-permute-done((bf16[4,8192]{1,0:T(4,128)(2,1)}, bf16[4,8192]{1,0:T(4,128)(2,1)S(1)}, u32[]{:S(2)}, u32[]{:S(2)}) %collective-permute-start) | collective-permute-done | bytes 65568 | tf_op jit(solution)/shard_map/ppermute | solution.py:29
  6.4 4.4 %collective-permute-done.1 = bf16[4,8192]{1,0:T(4,128)(2,1)S(1)} collective-permute-done((bf16[4,8192]{1,0:T(4,128)(2,1)}, bf16[4,8192]{1,0:T(4,128)(2,1)S(1)}, u32[]{:S(2)}, u32[]{:S(2)}) %collective-permute-start.1) | collective-permute-done | bytes 65568 | tf_op jit(solution)/shard_map/ppermute | solution.py:29
  11.0 1.6 %collective-permute-start.2 = (bf16[2,4,8192]{2,1,0:T(4,128)(2,1)S(1)}, bf16[2,4,8192]{2,1,0:T(4,128)(2,1)S(1)}, u32[]{:S(2)}, u32[]{:S(2)}) collective-permute-start(bf16[2,4,8192]{2,1,0:T(4,128)(2,1)S(1)} %pad_maximum_fusion), channel_id=1, source_target_pairs={{0,16},{2,6},{4,20},{6,10},{8,24},{10,14},{12,28},{14,2},{16,32},{... | collective-permute-start | bytes 393224 | tf_op jit(solution)/shard_map/ppermute | solution.py:29
  12.6 1.7 %collective-permute-start.3 = (bf16[2,4,8192]{2,1,0:T(4,128)(2,1)S(1)}, bf16[2,4,8192]{2,1,0:T(4,128)(2,1)S(1)}, u32[]{:S(2)}, u32[]{:S(2)}) collective-permute-start(bf16[2,4,8192]{2,1,0:T(4,128)(2,1)S(1)} %pad_maximum_fusion), channel_id=1, source_target_pairs={{0,48},{2,14},{4,52},{6,2},{8,56},{10,6},{12,60},{14,10},{16,0},{1... | collective-permute-start | bytes 393224 | tf_op jit(solution)/shard_map/ppermute | solution.py:29
  14.3 2.0 %collective-permute-start.4 = (bf16[2,4,8192]{2,1,0:T(4,128)(2,1)S(1)}, bf16[2,4,8192]{2,1,0:T(4,128)(2,1)S(1)}, u32[]{:S(2)}, u32[]{:S(2)}) collective-permute-start(bf16[2,4,8192]{2,1,0:T(4,128)(2,1)S(1)} %pad_maximum_fusion), channel_id=1, source_target_pairs={{0,32},{2,10},{4,36},{6,14},{8,40},{10,2},{12,44},{14,6},{16,48},{... | collective-permute-start | bytes 393224 | tf_op jit(solution)/shard_map/ppermute | solution.py:29
  17.6 3.1 %collective-permute-done.4 = bf16[2,4,8192]{2,1,0:T(4,128)(2,1)S(1)} collective-permute-done((bf16[2,4,8192]{2,1,0:T(4,128)(2,1)S(1)}, bf16[2,4,8192]{2,1,0:T(4,128)(2,1)S(1)}, u32[]{:S(2)}, u32[]{:S(2)}) %collective-permute-start.4) | collective-permute-done | bytes 131104 | tf_op jit(solution)/shard_map/ppermute | solution.py:29
  20.8 1.1 %collective-permute-start.5 = (bf16[8,4,8192]{2,1,0:T(4,128)(2,1)S(1)}, bf16[8,4,8192]{2,1,0:T(4,128)(2,1)S(1)}, u32[]{:S(2)}, u32[]{:S(2)}) collective-permute-start(bf16[8,4,8192]{2,1,0:T(4,128)(2,1)S(1)} %constant_dynamic-update-slice_fusion.refs_0_), channel_id=1, source_target_pairs={{0,4},{2,18},{4,8},{6,22},{8,12},{10,26},{12,0},{14,30},{16,20},{1... | collective-permute-start | bytes 1572872 | tf_op jit(solution)/shard_map/ppermute | solution.py:29
  21.9 2.2 %collective-permute-start.7 = (bf16[8,4,8192]{2,1,0:T(4,128)(2,1)S(1)}, bf16[8,4,8192]{2,1,0:T(4,128)(2,1)S(1)}, u32[]{:S(2)}, u32[]{:S(2)}) collective-permute-start(bf16[8,4,8192]{2,1,0:T(4,128)(2,1)S(1)} %constant_dynamic-update-slice_fusion.refs_0_), channel_id=1, source_target_pairs={{0,12},{2,50},{4,0},{6,54},{8,4},{10,58},{12,8},{14,62},{16,28},{1... | collective-permute-start | bytes 1572872 | tf_op jit(solution)/shard_map/ppermute | solution.py:29
  24.1 7.2 %collective-permute-done.5.refs_0_ = bf16[8,4,8192]{2,1,0:T(4,128)(2,1)S(1)} collective-permute-done((bf16[8,4,8192]{2,1,0:T(4,128)(2,1)S(1)}, bf16[8,4,8192]{2,1,0:T(4,128)(2,1)S(1)}, u32[]{:S(2)}, u32[]{:S(2)}) %collective-permute-start.5) | collective-permute-done | bytes 524320 | tf_op jit(solution)/shard_map/ppermute | solution.py:29
  31.8 1.4 %collective-permute-done.12.refs_2_ = bf16[8,4,8192]{2,1,0:T(4,128)(2,1)S(1)} collective-permute-done((bf16[8,4,8192]{2,1,0:T(4,128)(2,1)S(1)}, bf16[8,4,8192]{2,1,0:T(4,128)(2,1)S(1)}, u32[]{:S(2)}, u32[]{:S(2)}) %collective-permute-start.12) | collective-permute-done | bytes 524320 | tf_op jit(solution)/shard_map/ppermute | solution.py:29
  33.9 2.1 %copy-done = bf16[231,8192]{1,0:T(8,128)(2,1)S(1)} copy-done((bf16[231,8192]{1,0:T(8,128)(2,1)S(1)}, bf16[231,8192]{1,0:T(8,128)(2,1)}, u32[]{:S(2)}) %copy-start) | copy-done | bytes 3784728
  36.0 2.1 %copy-done.3 = bf16[231,8192]{1,0:T(8,128)(2,1)S(1)} copy-done((bf16[231,8192]{1,0:T(8,128)(2,1)S(1)}, bf16[231,8192]{1,0:T(8,128)(2,1)}, u32[]{:S(2)}) %copy-start.3) | copy-done | bytes 3784728
  38.1 2.1 %copy-done.6 = bf16[231,8192]{1,0:T(8,128)(2,1)S(1)} copy-done((bf16[231,8192]{1,0:T(8,128)(2,1)S(1)}, bf16[231,8192]{1,0:T(8,128)(2,1)}, u32[]{:S(2)}) %copy-start.6) | copy-done | bytes 3784728
  40.2 3.0 %shard_map.49 = (bf16[32,2,8192]{2,1,0:T(2,128)(2,1)S(1)}, f32[64,8192]{1,0:T(8,128)S(1)}) custom-call(bf16[8,4,8192]{2,1,0:T(4,128)(2,1)S(1)} %collective-permute-done.5.refs_0_, bf16[8,4,8192]{2,1,0:T(4,128)(2,1)S(1)} %collective-permute-done.7.refs_1_, bf16[8,4,8192]{2,1,0:T(4,128)(2,1)S(1)} %collective-permute-done.12.refs_2_, ...), custom_call_target="tpu_custom_call" | custom-call | tf_op jit(solution)/shard_map/pallas_call | solution.py:133
  43.4 2.2 %shard_map.50.hidden_ref = bf16[64,231]{1,0:T(8,128)(2,1)S(1)} custom-call(bf16[8,4,8192]{2,1,0:T(4,128)(2,1)S(1)} %constant_dynamic-update-slice_fusion.refs_0_, bf16[8,4,8192]{2,1,0:T(4,128)(2,1)S(1)} %collective-permute-done.15.refs_1_, bf16[231,8192]{1,0:T(8,128)(2,1)S(1)} %copy-done, bf16[231,8192]{1,0:T(8,128)(2,1)S(1)} %copy-done.3), custom_call_target="tpu_custom_call" | custom-call | tf_op jit(solution)/shard_map/pallas_call | solution.py:133
  47.0 2.6 %collective-permute-start.8 = (bf16[4,4,8192]{2,1,0:T(4,128)(2,1)S(1)}, bf16[4,4,8192]{2,1,0:T(4,128)(2,1)S(1)}, u32[]{:S(2)}, u32[]{:S(2)}) collective-permute-start(bf16[4,4,8192]{2,1,0:T(4,128)(2,1)S(1)} %slice.9), channel_id=1, source_target_pairs={{0,12},{2,50},{4,0},{6,54},{8,4},{10,58},{12,8},{14,62},{16,28},{1... | collective-permute-start | bytes 786440 | tf_op jit(solution)/shard_map/ppermute | solution.py:29
  49.8 3.7 %collective-permute-done.8.refs_1_ = bf16[4,4,8192]{2,1,0:T(4,128)(2,1)S(1)} collective-permute-done((bf16[4,4,8192]{2,1,0:T(4,128)(2,1)S(1)}, bf16[4,4,8192]{2,1,0:T(4,128)(2,1)S(1)}, u32[]{:S(2)}, u32[]{:S(2)}) %collective-permute-start.8) | collective-permute-done | bytes 262176 | tf_op jit(solution)/shard_map/ppermute | solution.py:29
  53.5 3.9 %collective-permute-done.6.refs_0_ = bf16[4,4,8192]{2,1,0:T(4,128)(2,1)S(1)} collective-permute-done((bf16[4,4,8192]{2,1,0:T(4,128)(2,1)S(1)}, bf16[4,4,8192]{2,1,0:T(4,128)(2,1)S(1)}, u32[]{:S(2)}, u32[]{:S(2)}) %collective-permute-start.6) | collective-permute-done | bytes 262176 | tf_op jit(solution)/shard_map/ppermute | solution.py:29
  58.2 1.5 %collective-permute-start.17 = (bf16[8,2,8192]{2,1,0:T(2,128)(2,1)S(1)}, bf16[8,2,8192]{2,1,0:T(2,128)(2,1)S(1)}, u32[]{:S(2)}, u32[]{:S(2)}) collective-permute-start(bf16[8,2,8192]{2,1,0:T(2,128)(2,1)S(1)} %get-tuple-element.19), channel_id=1, source_target_pairs={{0,4},{2,18},{4,8},{6,22},{8,12},{10,26},{12,0},{14,30},{16,20},{1... | collective-permute-start | bytes 786440 | tf_op jit(solution)/shard_map/ppermute | solution.py:29
  59.7 3.0 %shard_map.48 = (bf16[16,2,8192]{2,1,0:T(2,128)(2,1)S(1)}, f32[32,8192]{1,0:T(8,128)S(1)}) custom-call(bf16[4,4,8192]{2,1,0:T(4,128)(2,1)S(1)} %collective-permute-done.6.refs_0_, bf16[4,4,8192]{2,1,0:T(4,128)(2,1)S(1)} %collective-permute-done.8.refs_1_, bf16[4,4,8192]{2,1,0:T(4,128)(2,1)S(1)} %collective-permute-done.9.refs_2_, ...), custom_call_target="tpu_custom_call" | custom-call | tf_op jit(solution)/shard_map/pallas_call | solution.py:133
  62.9 1.2 %collective-permute-done.19.lent_ref = bf16[8,2,8192]{2,1,0:T(2,128)(2,1)S(1)} collective-permute-done((bf16[8,2,8192]{2,1,0:T(2,128)(2,1)S(1)}, bf16[8,2,8192]{2,1,0:T(2,128)(2,1)S(1)}, u32[]{:S(2)}, u32[]{:S(2)}) %collective-permute-start.19) | collective-permute-done | bytes 262176 | tf_op jit(solution)/shard_map/ppermute | solution.py:29
  64.4 1.8 %collective-permute-start.20 = (bf16[16,2,8192]{2,1,0:T(2,128)(2,1)S(1)}, bf16[16,2,8192]{2,1,0:T(2,128)(2,1)S(1)}, u32[]{:S(2)}, u32[]{:S(2)}) collective-permute-start(bf16[16,2,8192]{2,1,0:T(2,128)(2,1)S(1)} %shard_map.54), channel_id=1, source_target_pairs={{0,12},{2,50},{4,0},{6,54},{8,4},{10,58},{12,8},{14,62},{16,28},{1... | collective-permute-start | bytes 1572872 | tf_op jit(solution)/shard_map/ppermute | solution.py:29
  66.9 6.7 %collective-permute-done.20.high_ref = bf16[16,2,8192]{2,1,0:T(2,128)(2,1)S(1)} collective-permute-done((bf16[16,2,8192]{2,1,0:T(2,128)(2,1)S(1)}, bf16[16,2,8192]{2,1,0:T(2,128)(2,1)S(1)}, u32[]{:S(2)}, u32[]{:S(2)}) %collective-permute-start.20) | collective-permute-done | bytes 524320 | tf_op jit(solution)/shard_map/ppermute | solution.py:29
  73.7 3.3 %collective-permute-done.18.low_ref = bf16[16,2,8192]{2,1,0:T(2,128)(2,1)S(1)} collective-permute-done((bf16[16,2,8192]{2,1,0:T(2,128)(2,1)S(1)}, bf16[16,2,8192]{2,1,0:T(2,128)(2,1)S(1)}, u32[]{:S(2)}, u32[]{:S(2)}) %collective-permute-start.18) | collective-permute-done | bytes 524320 | tf_op jit(solution)/shard_map/ppermute | solution.py:29
  77.0 1.4 %shard_map.55 = bf16[16,2,8192]{2,1,0:T(2,128)(2,1)} custom-call(f32[32,8192]{1,0:T(8,128)S(1)} %get-tuple-element.13.own_ref, bf16[16,2,8192]{2,1,0:T(2,128)(2,1)S(1)} %collective-permute-done.11.fold_ref, bf16[16,2,8192]{2,1,0:T(2,128)(2,1)S(1)} %collective-permute-done.18.low_ref, bf16[16,2,8192]{2,1,0:T(2,128)(2,1)S(1)} %collective-permute-done.20.high_ref), custom_call_target="tpu_custom_call" | custom-call | tf_op jit(solution)/shard_map/pallas_call | solution.py:133
  78.4 5.8 %all-to-all-start = ((bf16[16,2,8192]{2,1,0:T(2,128)(2,1)}), bf16[16,2,8192]{2,1,0:T(2,128)(2,1)S(1)}, u32[]{:S(2)}, u32[]{:S(2)}) async-start(bf16[16,2,8192]{2,1,0:T(2,128)(2,1)} %shard_map.55), calls=%async_computation | async-start | bytes 1048576 | tf_op jit(solution)/shard_map/all_to_all | solution.py:232
  84.2 2.1 %copy-done.2 = bf16[231,8192]{1,0:T(8,128)(2,1)S(1)} copy-done((bf16[231,8192]{1,0:T(8,128)(2,1)S(1)}, bf16[231,8192]{1,0:T(8,128)(2,1)}, u32[]{:S(2)}) %copy-start.2) | copy-done | bytes 3784728
  86.9 1.5 %copy-done.5 = bf16[231,8192]{1,0:T(8,128)(2,1)S(1)} copy-done((bf16[231,8192]{1,0:T(8,128)(2,1)S(1)}, bf16[231,8192]{1,0:T(8,128)(2,1)}, u32[]{:S(2)}) %copy-start.5) | copy-done | bytes 3784728
  89.0 4.9 %all-to-all-done = bf16[16,2,8192]{2,1,0:T(2,128)(2,1)S(1)} async-done(((bf16[16,2,8192]{2,1,0:T(2,128)(2,1)}), bf16[16,2,8192]{2,1,0:T(2,128)(2,1)S(1)}, u32[]{:S(2)}, u32[]{:S(2)}) %all-to-all-start) | async-done | bytes 524320 | tf_op jit(solution)/shard_map/all_to_all | solution.py:232
  93.9 1.1 %reduce_sum.12 = bf16[2,8192]{1,0:T(2,128)(2,1)} reduce(bf16[16,2,8192]{2,1,0:T(2,128)(2,1)S(1)} %all-to-all-done, bf16[]{:T(256)} %constant.2.clone.1), dimensions={0}, to_apply=%region_0.0 | reduce | flops 245760 | bytes 557058 | tf_op jit(solution)/shard_map/reduce_sum | solution.py:235
  (47 shorter events, 7.8 us)
Async XLA Ops:
  0.0 6.4 %collective-permute-start = (bf16[4,8192]{1,0:T(4,128)(2,1)}, bf16[4,8192]{1,0:T(4,128)(2,1)S(1)}, u32[]{:S(2)}, u32[]{:S(2)}) collective-permute-start(bf16[4,8192]{1,0:T(4,128)(2,1)} %param.4), channel_id=1, source_target_pairs={{0,8},{2,34},{4,12},{6,38},{8,0},{10,42},{12,4},{14,46},{16,24},{1... | collective-permute-start | bytes 196616 | tf_op jit(solution)/shard_map/ppermute | solution.py:29
  4.0 6.9 %collective-permute-start.1 = (bf16[4,8192]{1,0:T(4,128)(2,1)}, bf16[4,8192]{1,0:T(4,128)(2,1)S(1)}, u32[]{:S(2)}, u32[]{:S(2)}) collective-permute-start(bf16[4,8192]{1,0:T(4,128)(2,1)} %param.4), channel_id=1, source_target_pairs={{0,72},{2,98},{4,76},{6,102},{8,64},{10,106},{12,68},{14,110},{16,... | collective-permute-start | bytes 196616 | tf_op jit(solution)/shard_map/ppermute | solution.py:29
  11.0 6.2 %collective-permute-start.2 = (bf16[2,4,8192]{2,1,0:T(4,128)(2,1)S(1)}, bf16[2,4,8192]{2,1,0:T(4,128)(2,1)S(1)}, u32[]{:S(2)}, u32[]{:S(2)}) collective-permute-start(bf16[2,4,8192]{2,1,0:T(4,128)(2,1)S(1)} %pad_maximum_fusion), channel_id=1, source_target_pairs={{0,16},{2,6},{4,20},{6,10},{8,24},{10,14},{12,28},{14,2},{16,32},{... | collective-permute-start | bytes 393224 | tf_op jit(solution)/shard_map/ppermute | solution.py:29
  12.6 5.0 %collective-permute-start.3 = (bf16[2,4,8192]{2,1,0:T(4,128)(2,1)S(1)}, bf16[2,4,8192]{2,1,0:T(4,128)(2,1)S(1)}, u32[]{:S(2)}, u32[]{:S(2)}) collective-permute-start(bf16[2,4,8192]{2,1,0:T(4,128)(2,1)S(1)} %pad_maximum_fusion), channel_id=1, source_target_pairs={{0,48},{2,14},{4,52},{6,2},{8,56},{10,6},{12,60},{14,10},{16,0},{1... | collective-permute-start | bytes 393224 | tf_op jit(solution)/shard_map/ppermute | solution.py:29
  14.3 6.5 %collective-permute-start.4 = (bf16[2,4,8192]{2,1,0:T(4,128)(2,1)S(1)}, bf16[2,4,8192]{2,1,0:T(4,128)(2,1)S(1)}, u32[]{:S(2)}, u32[]{:S(2)}) collective-permute-start(bf16[2,4,8192]{2,1,0:T(4,128)(2,1)S(1)} %pad_maximum_fusion), channel_id=1, source_target_pairs={{0,32},{2,10},{4,36},{6,14},{8,40},{10,2},{12,44},{14,6},{16,48},{... | collective-permute-start | bytes 393224 | tf_op jit(solution)/shard_map/ppermute | solution.py:29
  20.8 10.5 %collective-permute-start.5 = (bf16[8,4,8192]{2,1,0:T(4,128)(2,1)S(1)}, bf16[8,4,8192]{2,1,0:T(4,128)(2,1)S(1)}, u32[]{:S(2)}, u32[]{:S(2)}) collective-permute-start(bf16[8,4,8192]{2,1,0:T(4,128)(2,1)S(1)} %constant_dynamic-update-slice_fusion.refs_0_), channel_id=1, source_target_pairs={{0,4},{2,18},{4,8},{6,22},{8,12},{10,26},{12,0},{14,30},{16,20},{1... | collective-permute-start | bytes 1572872 | tf_op jit(solution)/shard_map/ppermute | solution.py:29
  21.9 9.4 %collective-permute-start.7 = (bf16[8,4,8192]{2,1,0:T(4,128)(2,1)S(1)}, bf16[8,4,8192]{2,1,0:T(4,128)(2,1)S(1)}, u32[]{:S(2)}, u32[]{:S(2)}) collective-permute-start(bf16[8,4,8192]{2,1,0:T(4,128)(2,1)S(1)} %constant_dynamic-update-slice_fusion.refs_0_), channel_id=1, source_target_pairs={{0,12},{2,50},{4,0},{6,54},{8,4},{10,58},{12,8},{14,62},{16,28},{1... | collective-permute-start | bytes 1572872 | tf_op jit(solution)/shard_map/ppermute | solution.py:29
  31.3 1.9 %collective-permute-start.12 = (bf16[8,4,8192]{2,1,0:T(4,128)(2,1)S(1)}, bf16[8,4,8192]{2,1,0:T(4,128)(2,1)S(1)}, u32[]{:S(2)}, u32[]{:S(2)}) collective-permute-start(bf16[8,4,8192]{2,1,0:T(4,128)(2,1)S(1)} %collective-permute-done.5.refs_0_), channel_id=1, source_target_pairs={{0,2},{2,0},{4,6},{6,4},{8,10},{10,8},{12,14},{14,12},{16,18},{18,... | collective-permute-start | bytes 1572872 | tf_op jit(solution)/shard_map/ppermute | solution.py:29
  31.3 2.7 %collective-permute-start.13 = (bf16[8,4,8192]{2,1,0:T(4,128)(2,1)S(1)}, bf16[8,4,8192]{2,1,0:T(4,128)(2,1)S(1)}, u32[]{:S(2)}, u32[]{:S(2)}) collective-permute-start(bf16[8,4,8192]{2,1,0:T(4,128)(2,1)S(1)} %collective-permute-done.7.refs_1_), channel_id=1, source_target_pairs={{0,2},{2,0},{4,6},{6,4},{8,10},{10,8},{12,14},{14,12},{16,18},{18,... | collective-permute-start | bytes 1572872 | tf_op jit(solution)/shard_map/ppermute | solution.py:29
  31.8 11.6 %collective-permute-start.15 = (bf16[8,4,8192]{2,1,0:T(4,128)(2,1)S(1)}, bf16[8,4,8192]{2,1,0:T(4,128)(2,1)S(1)}, u32[]{:S(2)}, u32[]{:S(2)}) collective-permute-start(bf16[8,4,8192]{2,1,0:T(4,128)(2,1)S(1)} %constant_dynamic-update-slice_fusion.refs_0_), channel_id=1, source_target_pairs={{0,2},{2,0},{4,6},{6,4},{8,10},{10,8},{12,14},{14,12},{16,18},{18,... | collective-permute-start | bytes 1572872 | tf_op jit(solution)/shard_map/ppermute | solution.py:29
  33.9 2.1 %copy-start = (bf16[231,8192]{1,0:T(8,128)(2,1)S(1)}, bf16[231,8192]{1,0:T(8,128)(2,1)}, u32[]{:S(2)}) copy-start(bf16[231,8192]{1,0:T(8,128)(2,1)} %refs_2_.1) | copy-start | bytes 11354116
  36.0 2.1 %copy-start.3 = (bf16[231,8192]{1,0:T(8,128)(2,1)S(1)}, bf16[231,8192]{1,0:T(8,128)(2,1)}, u32[]{:S(2)}) copy-start(bf16[231,8192]{1,0:T(8,128)(2,1)} %refs_3_.1) | copy-start | bytes 11354116
  38.1 2.1 %copy-start.6 = (bf16[231,8192]{1,0:T(8,128)(2,1)S(1)}, bf16[231,8192]{1,0:T(8,128)(2,1)}, u32[]{:S(2)}) copy-start(bf16[231,8192]{1,0:T(8,128)(2,1)} %refs_0_.5) | copy-start | bytes 11354116
  43.2 2.5 %copy-start.7 = (bf16[231,8192]{1,0:T(8,128)(2,1)S(1)}, bf16[231,8192]{1,0:T(8,128)(2,1)}, u32[]{:S(2)}) copy-start(bf16[231,8192]{1,0:T(8,128)(2,1)} %refs_0_.5) | copy-start | bytes 11354116
  43.2 20.9 %collective-permute-start.14 = (bf16[32,2,8192]{2,1,0:T(2,128)(2,1)S(1)}, bf16[32,2,8192]{2,1,0:T(2,128)(2,1)S(1)}, u32[]{:S(2)}, u32[]{:S(2)}) collective-permute-start(bf16[32,2,8192]{2,1,0:T(2,128)(2,1)S(1)} %get-tuple-element.16), channel_id=1, source_target_pairs={{0,2},{2,0},{4,6},{6,4},{8,10},{10,8},{12,14},{14,12},{16,18},{18,... | collective-permute-start | bytes 3145736 | tf_op jit(solution)/shard_map/ppermute | solution.py:29
  43.4 16.3 %copy-start.4 = (bf16[231,8192]{1,0:T(8,128)(2,1)S(1)}, bf16[231,8192]{1,0:T(8,128)(2,1)}, u32[]{:S(2)}) copy-start(bf16[231,8192]{1,0:T(8,128)(2,1)} %refs_3_.1) | copy-start | bytes 11354116
  45.7 14.1 %copy-start.1 = (bf16[231,8192]{1,0:T(8,128)(2,1)S(1)}, bf16[231,8192]{1,0:T(8,128)(2,1)}, u32[]{:S(2)}) copy-start(bf16[231,8192]{1,0:T(8,128)(2,1)} %refs_2_.1) | copy-start | bytes 11354116
  46.5 10.9 %collective-permute-start.16 = (bf16[16,2,8192]{2,1,0:T(2,128)(2,1)S(1)}, bf16[16,2,8192]{2,1,0:T(2,128)(2,1)S(1)}, u32[]{:S(2)}, u32[]{:S(2)}) collective-permute-start(bf16[16,2,8192]{2,1,0:T(2,128)(2,1)S(1)} %get-tuple-element.18), channel_id=1, source_target_pairs={{0,2},{2,0},{4,6},{6,4},{8,10},{10,8},{12,14},{14,12},{16,18},{18,... | collective-permute-start | bytes 1572872 | tf_op jit(solution)/shard_map/ppermute | solution.py:29
  47.0 6.5 %collective-permute-start.8 = (bf16[4,4,8192]{2,1,0:T(4,128)(2,1)S(1)}, bf16[4,4,8192]{2,1,0:T(4,128)(2,1)S(1)}, u32[]{:S(2)}, u32[]{:S(2)}) collective-permute-start(bf16[4,4,8192]{2,1,0:T(4,128)(2,1)S(1)} %slice.9), channel_id=1, source_target_pairs={{0,12},{2,50},{4,0},{6,54},{8,4},{10,58},{12,8},{14,62},{16,28},{1... | collective-permute-start | bytes 786440 | tf_op jit(solution)/shard_map/ppermute | solution.py:29
  49.7 7.7 %collective-permute-start.6 = (bf16[4,4,8192]{2,1,0:T(4,128)(2,1)S(1)}, bf16[4,4,8192]{2,1,0:T(4,128)(2,1)S(1)}, u32[]{:S(2)}, u32[]{:S(2)}) collective-permute-start(bf16[4,4,8192]{2,1,0:T(4,128)(2,1)S(1)} %slice.8), channel_id=1, source_target_pairs={{0,4},{2,18},{4,8},{6,22},{8,12},{10,26},{12,0},{14,30},{16,20},{1... | collective-permute-start | bytes 786440 | tf_op jit(solution)/shard_map/ppermute | solution.py:29
  53.5 6.2 %collective-permute-start.10 = (bf16[4,4,8192]{2,1,0:T(4,128)(2,1)S(1)}, bf16[4,4,8192]{2,1,0:T(4,128)(2,1)S(1)}, u32[]{:S(2)}, u32[]{:S(2)}) collective-permute-start(bf16[4,4,8192]{2,1,0:T(4,128)(2,1)S(1)} %collective-permute-done.8.refs_1_), channel_id=1, source_target_pairs={{0,2},{2,0},{4,6},{6,4},{8,10},{10,8},{12,14},{14,12},{16,18},{18,... | collective-permute-start | bytes 786440 | tf_op jit(solution)/shard_map/ppermute | solution.py:29
  57.4 2.4 %collective-permute-start.9 = (bf16[4,4,8192]{2,1,0:T(4,128)(2,1)S(1)}, bf16[4,4,8192]{2,1,0:T(4,128)(2,1)S(1)}, u32[]{:S(2)}, u32[]{:S(2)}) collective-permute-start(bf16[4,4,8192]{2,1,0:T(4,128)(2,1)S(1)} %collective-permute-done.6.refs_0_), channel_id=1, source_target_pairs={{0,2},{2,0},{4,6},{6,4},{8,10},{10,8},{12,14},{14,12},{16,18},{18,... | collective-permute-start | bytes 786440 | tf_op jit(solution)/shard_map/ppermute | solution.py:29
  57.6 6.4 %collective-permute-start.19 = (bf16[8,2,8192]{2,1,0:T(2,128)(2,1)S(1)}, bf16[8,2,8192]{2,1,0:T(2,128)(2,1)S(1)}, u32[]{:S(2)}, u32[]{:S(2)}) collective-permute-start(bf16[8,2,8192]{2,1,0:T(2,128)(2,1)S(1)} %get-tuple-element.20), channel_id=1, source_target_pairs={{0,12},{2,50},{4,0},{6,54},{8,4},{10,58},{12,8},{14,62},{16,28},{1... | collective-permute-start | bytes 786440 | tf_op jit(solution)/shard_map/ppermute | solution.py:29
  58.2 8.0 %collective-permute-start.17 = (bf16[8,2,8192]{2,1,0:T(2,128)(2,1)S(1)}, bf16[8,2,8192]{2,1,0:T(2,128)(2,1)S(1)}, u32[]{:S(2)}, u32[]{:S(2)}) collective-permute-start(bf16[8,2,8192]{2,1,0:T(2,128)(2,1)S(1)} %get-tuple-element.19), channel_id=1, source_target_pairs={{0,4},{2,18},{4,8},{6,22},{8,12},{10,26},{12,0},{14,30},{16,20},{1... | collective-permute-start | bytes 786440 | tf_op jit(solution)/shard_map/ppermute | solution.py:29
  62.8 4.1 %collective-permute-start.11 = (bf16[16,2,8192]{2,1,0:T(2,128)(2,1)S(1)}, bf16[16,2,8192]{2,1,0:T(2,128)(2,1)S(1)}, u32[]{:S(2)}, u32[]{:S(2)}) collective-permute-start(bf16[16,2,8192]{2,1,0:T(2,128)(2,1)S(1)} %get-tuple-element.14), channel_id=1, source_target_pairs={{0,2},{2,0},{4,6},{6,4},{8,10},{10,8},{12,14},{14,12},{16,18},{18,... | collective-permute-start | bytes 1572872 | tf_op jit(solution)/shard_map/ppermute | solution.py:29
  64.4 9.3 %collective-permute-start.20 = (bf16[16,2,8192]{2,1,0:T(2,128)(2,1)S(1)}, bf16[16,2,8192]{2,1,0:T(2,128)(2,1)S(1)}, u32[]{:S(2)}, u32[]{:S(2)}) collective-permute-start(bf16[16,2,8192]{2,1,0:T(2,128)(2,1)S(1)} %shard_map.54), channel_id=1, source_target_pairs={{0,12},{2,50},{4,0},{6,54},{8,4},{10,58},{12,8},{14,62},{16,28},{1... | collective-permute-start | bytes 1572872 | tf_op jit(solution)/shard_map/ppermute | solution.py:29
  66.5 10.5 %collective-permute-start.18 = (bf16[16,2,8192]{2,1,0:T(2,128)(2,1)S(1)}, bf16[16,2,8192]{2,1,0:T(2,128)(2,1)S(1)}, u32[]{:S(2)}, u32[]{:S(2)}) collective-permute-start(bf16[16,2,8192]{2,1,0:T(2,128)(2,1)S(1)} %shard_map.53), channel_id=1, source_target_pairs={{0,4},{2,18},{4,8},{6,22},{8,12},{10,26},{12,0},{14,30},{16,20},{1... | collective-permute-start | bytes 1572872 | tf_op jit(solution)/shard_map/ppermute | solution.py:29
  78.4 15.5 %all-to-all-start = ((bf16[16,2,8192]{2,1,0:T(2,128)(2,1)}), bf16[16,2,8192]{2,1,0:T(2,128)(2,1)S(1)}, u32[]{:S(2)}, u32[]{:S(2)}) async-start(bf16[16,2,8192]{2,1,0:T(2,128)(2,1)} %shard_map.55), calls=%async_computation | async-start | bytes 1048576 | tf_op jit(solution)/shard_map/all_to_all | solution.py:232
  84.2 2.1 %copy-start.2 = (bf16[231,8192]{1,0:T(8,128)(2,1)S(1)}, bf16[231,8192]{1,0:T(8,128)(2,1)}, u32[]{:S(2)}) copy-start(bf16[231,8192]{1,0:T(8,128)(2,1)} %refs_2_.1) | copy-start | bytes 11354116
  86.3 2.1 %copy-start.5 = (bf16[231,8192]{1,0:T(8,128)(2,1)S(1)}, bf16[231,8192]{1,0:T(8,128)(2,1)}, u32[]{:S(2)}) copy-start(bf16[231,8192]{1,0:T(8,128)(2,1)} %refs_3_.1) | copy-start | bytes 11354116
where the time goes:
time: 95.3 us; the launch traced here: 95 us
  waiting for transfers between devices  43.3 us (45%)
  starting transfers between devices  27.4 us (29%)
  Pallas kernels  12.7 us (13%)
  local copies, waits for them, and re-layouts  10.2 us (11%)
  other arithmetic  1.16 us (1%)
    ppermute x21, waiting for transfers between devices, move(): return lax.ppermute(v, ALL, pairs)  38.4 us
    ppermute x21, starting transfers between devices, move(): return lax.ppermute(v, ALL, pairs)  21.7 us
    pallas_call x8, Pallas kernels, call(): pl.pallas_call(kernel, out_shape=shapes, in_specs=[VM] * len(args), out_s...  11.5 us
    unnamed x20, local copies, waits for them, and re-layouts  9.99 us
    all_to_all x1, starting transfers between devices, per_device(): lax.all_to_all(part, ALL, 0, 0, axis_index_groups=plane_groups(), tiled=T...  5.77 us
    all_to_all x1, waiting for transfers between devices, per_device(): lax.all_to_all(part, ALL, 0, 0, axis_index_groups=plane_groups(), tiled=T...  4.93 us
  transfers between devices with their start and end apart: 22, of which 14 were waited for; matrix products, arithmetic and copies ran while one was open for 0% of the time, Pallas kernels for 12%

commit v1 on v0

--- a/solution.py
+++ b/solution.py
@@ -90,20 +90,25 @@
     hidden_ref[...] = hidden_of(x_refs, gate_ref, up_ref)
 
 
-def work_kernel(*refs):
-    *x_refs, gate_ref, up_ref, down_ref, sib_ref, own_ref = refs
-    down_rows(hidden_of(x_refs, gate_ref, up_ref), down_ref, sib_ref, own_ref)
+def work_kernel(pieces, *refs):
+    *x_refs, gate_ref, up_ref, down_ref = refs[: -pieces - 1]
+    hidden = hidden_of(x_refs, gate_ref, up_ref)
+    down_rows(hidden, down_ref, *refs[-pieces - 1 :])
 
 
 def down_kernel(hidden_ref, *refs):
     down_rows(hidden_ref[...], *refs)
 
 
-def down_rows(hidden, down_ref, sib_ref, own_ref):
+def down_rows(hidden, down_ref, *outs):
     part = jnp.dot(hidden, down_ref[...], preferred_element_type=F32)
-    rows = own_ref.shape[0]
-    own_ref[...] = part[:rows]
-    sib_ref[...] = part[rows:].astype(BF).reshape(sib_ref.shape)
+    *sib_refs, own_ref = outs
+    at = own_ref.shape[0]
+    own_ref[...] = part[:at]
+    for sib_ref in sib_refs:
+        rows = sib_ref.shape[0] * 2
+        sib_ref[...] = part[at : at + rows].astype(BF).reshape(sib_ref.shape)
+        at += rows
 
 
 def add_kernel(own_ref, fold_ref, *outs):
@@ -118,7 +123,7 @@
     n = out_ref.shape[0]
     d = own_ref.shape[1]
     part = own_ref[2 * n * which : 2 * n * (which + 1), :]
-    part += fold_ref[n * which : n * (which + 1)].reshape(-1, d).astype(F32)
+    part += fold_ref[...].reshape(-1, d).astype(F32)
     lent = part[n * which : n * (which + 1)] + lent_ref[...].reshape(n, d).astype(F32)
     kept = part[n * (1 - which) : n * (2 - which)]
     h = n // 2
@@ -143,11 +148,12 @@
     return jax.ShapeDtypeStruct((blocks, 2, d), BF)
 
 
-def work(weights, *xs):
+def work(weights, *xs, pieces=1):
     d = xs[0].shape[2]
     rows = sum(x.shape[0] * x.shape[1] for x in xs) // 2
-    shapes = [piece(rows // 2, d), jax.ShapeDtypeStruct((rows, d), F32)]
-    return call(work_kernel, shapes, *xs, *weights)
+    shapes = [piece(rows // 2 // pieces, d)] * pieces
+    shapes.append(jax.ShapeDtypeStruct((rows, d), F32))
+    return call(functools.partial(work_kernel, pieces), shapes, *xs, *weights)
 
 
 def add(outs, own, *pieces):
@@ -213,14 +219,15 @@
     high_sib = core(high)
     own_a = ring(low[:4], 1)
     own_b = ring(high[4:], -1)
-    part, own_part = work(weights, low, high, low_sib, high_sib)
-    part = core(part)
+    for_low, for_high, own_part = work(weights, low, high, low_sib, high_sib, pieces=2)
+    fold_low = core(for_low)
+    fold_high = core(for_high)
     (part_low,) = call(
-        functools.partial(ring_kernel, 0), [piece(16, d)], own_part, part, lent_low
+        functools.partial(ring_kernel, 0), [piece(16, d)], own_part, fold_low, lent_low
     )
     back_low = ring(part_low, 1)
     (part_high,) = call(
-        functools.partial(ring_kernel, 1), [piece(16, d)], own_part, part, lent_high
+        functools.partial(ring_kernel, 1), [piece(16, d)], own_part, fold_high, lent_high
     )
     back_high = ring(part_high, -1)
 

time: 95.3 us -> 88.3 us (0.927)
  waiting for transfers between devices: 43.3 us -> 37.4 us
  local copies, waits for them, and re-layouts: 10.2 us -> 8.16 us
    ppermute x21 -> x22, waiting for transfers between devices: 38.4 us -> 32.5 us  [move(): return lax.ppermute(v, ALL, pairs)]
    unnamed x20 -> x18, local copies, waits for them, and re-layouts: 9.99 us -> 7.91 us
    ppermute x21 -> x22, starting transfers between devices: 21.7 us -> 22.4 us  [move(): return lax.ppermute(v, ALL, pairs)]
  transfers between devices with their start and end apart: 22 -> 23, of which waited for: 14 -> 12; matrix products, arithmetic and copies ran while one was open for 0% -> 0% of each run, Pallas kernels for 12% -> 13%
where the time goes in v1:
time: 88.3 us; the launch traced here: 87.9 us
  waiting for transfers between devices  37.4 us (42%)
  starting transfers between devices  28.3 us (32%)
  Pallas kernels  12.6 us (14%)
  local copies, waits for them, and re-layouts  8.16 us (9%)
  other arithmetic  1.16 us (1%)
    ppermute x22, waiting for transfers between devices, move(): return lax.ppermute(v, ALL, pairs)  32.5 us
    ppermute x22, starting transfers between devices, move(): return lax.ppermute(v, ALL, pairs)  22.4 us
    pallas_call x8, Pallas kernels, call(): pl.pallas_call(kernel, out_shape=shapes, in_specs=[VM] * len(args), out_s...  11.5 us
    unnamed x18, local copies, waits for them, and re-layouts  7.91 us
    all_to_all x1, starting transfers between devices, per_device(): lax.all_to_all(part, ALL, 0, 0, axis_index_groups=plane_groups(), tiled=T...  5.9 us
    all_to_all x1, waiting for transfers between devices, per_device(): lax.all_to_all(part, ALL, 0, 0, axis_index_groups=plane_groups(), tiled=T...  4.93 us
  transfers between devices with their start and end apart: 23, of which 12 were waited for; matrix products, arithmetic and copies ran while one was open for 0% of the time, Pallas kernels for 13%

profile of v1, /device:TPU:0, one launch (start us, length us, event | category | flops | bytes accessed | tf_op | source)
XLA Modules:
  0.0 87.9 jit_solution(2701310709036951552)
XLA Ops:
  0.0 4.0 %collective-permute-start = (bf16[4,8192]{1,0:T(4,128)(2,1)}, bf16[4,8192]{1,0:T(4,128)(2,1)S(1)}, u32[]{:S(2)}, u32[]{:S(2)}) collective-permute-start(bf16[4,8192]{1,0:T(4,128)(2,1)} %param.4), channel_id=1, source_target_pairs={{0,8},{2,34},{4,12},{6,38},{8,0},{10,42},{12,4},{14,46},{16,24},{1... | collective-permute-start | bytes 196616 | tf_op jit(solution)/shard_map/ppermute | solution.py:29
  4.0 0.9 %collective-permute-start.1 = (bf16[4,8192]{1,0:T(4,128)(2,1)}, bf16[4,8192]{1,0:T(4,128)(2,1)S(1)}, u32[]{:S(2)}, u32[]{:S(2)}) collective-permute-start(bf16[4,8192]{1,0:T(4,128)(2,1)} %param.4), channel_id=1, source_target_pairs={{0,72},{2,98},{4,76},{6,102},{8,64},{10,106},{12,68},{14,110},{16,... | collective-permute-start | bytes 196616 | tf_op jit(solution)/shard_map/ppermute | solution.py:29
  4.9 1.5 %collective-permute-done = bf16[4,8192]{1,0:T(4,128)(2,1)S(1)} collective-permute-done((bf16[4,8192]{1,0:T(4,128)(2,1)}, bf16[4,8192]{1,0:T(4,128)(2,1)S(1)}, u32[]{:S(2)}, u32[]{:S(2)}) %collective-permute-start) | collective-permute-done | bytes 65568 | tf_op jit(solution)/shard_map/ppermute | solution.py:29
  6.4 4.4 %collective-permute-done.1 = bf16[4,8192]{1,0:T(4,128)(2,1)S(1)} collective-permute-done((bf16[4,8192]{1,0:T(4,128)(2,1)}, bf16[4,8192]{1,0:T(4,128)(2,1)S(1)}, u32[]{:S(2)}, u32[]{:S(2)}) %collective-permute-start.1) | collective-permute-done | bytes 65568 | tf_op jit(solution)/shard_map/ppermute | solution.py:29
  11.0 1.6 %collective-permute-start.2 = (bf16[2,4,8192]{2,1,0:T(4,128)(2,1)S(1)}, bf16[2,4,8192]{2,1,0:T(4,128)(2,1)S(1)}, u32[]{:S(2)}, u32[]{:S(2)}) collective-permute-start(bf16[2,4,8192]{2,1,0:T(4,128)(2,1)S(1)} %pad_maximum_fusion), channel_id=1, source_target_pairs={{0,16},{2,6},{4,20},{6,10},{8,24},{10,14},{12,28},{14,2},{16,32},{... | collective-permute-start | bytes 393224 | tf_op jit(solution)/shard_map/ppermute | solution.py:29
  12.6 1.7 %collective-permute-start.3 = (bf16[2,4,8192]{2,1,0:T(4,128)(2,1)S(1)}, bf16[2,4,8192]{2,1,0:T(4,128)(2,1)S(1)}, u32[]{:S(2)}, u32[]{:S(2)}) collective-permute-start(bf16[2,4,8192]{2,1,0:T(4,128)(2,1)S(1)} %pad_maximum_fusion), channel_id=1, source_target_pairs={{0,48},{2,14},{4,52},{6,2},{8,56},{10,6},{12,60},{14,10},{16,0},{1... | collective-permute-start | bytes 393224 | tf_op jit(solution)/shard_map/ppermute | solution.py:29
  14.3 2.0 %collective-permute-start.4 = (bf16[2,4,8192]{2,1,0:T(4,128)(2,1)S(1)}, bf16[2,4,8192]{2,1,0:T(4,128)(2,1)S(1)}, u32[]{:S(2)}, u32[]{:S(2)}) collective-permute-start(bf16[2,4,8192]{2,1,0:T(4,128)(2,1)S(1)} %pad_maximum_fusion), channel_id=1, source_target_pairs={{0,32},{2,10},{4,36},{6,14},{8,40},{10,2},{12,44},{14,6},{16,48},{... | collective-permute-start | bytes 393224 | tf_op jit(solution)/shard_map/ppermute | solution.py:29
  16.3 0.9 %collective-permute-done.2 = bf16[2,4,8192]{2,1,0:T(4,128)(2,1)S(1)} collective-permute-done((bf16[2,4,8192]{2,1,0:T(4,128)(2,1)S(1)}, bf16[2,4,8192]{2,1,0:T(4,128)(2,1)S(1)}, u32[]{:S(2)}, u32[]{:S(2)}) %collective-permute-start.2) | collective-permute-done | bytes 131104 | tf_op jit(solution)/shard_map/ppermute | solution.py:29
  17.6 3.1 %collective-permute-done.4 = bf16[2,4,8192]{2,1,0:T(4,128)(2,1)S(1)} collective-permute-done((bf16[2,4,8192]{2,1,0:T(4,128)(2,1)S(1)}, bf16[2,4,8192]{2,1,0:T(4,128)(2,1)S(1)}, u32[]{:S(2)}, u32[]{:S(2)}) %collective-permute-start.4) | collective-permute-done | bytes 131104 | tf_op jit(solution)/shard_map/ppermute | solution.py:29
  20.8 1.1 %collective-permute-start.5 = (bf16[8,4,8192]{2,1,0:T(4,128)(2,1)S(1)}, bf16[8,4,8192]{2,1,0:T(4,128)(2,1)S(1)}, u32[]{:S(2)}, u32[]{:S(2)}) collective-permute-start(bf16[8,4,8192]{2,1,0:T(4,128)(2,1)S(1)} %constant_dynamic-update-slice_fusion.refs_0_), channel_id=1, source_target_pairs={{0,4},{2,18},{4,8},{6,22},{8,12},{10,26},{12,0},{14,30},{16,20},{1... | collective-permute-start | bytes 1572872 | tf_op jit(solution)/shard_map/ppermute | solution.py:29
  21.9 2.2 %collective-permute-start.7 = (bf16[8,4,8192]{2,1,0:T(4,128)(2,1)S(1)}, bf16[8,4,8192]{2,1,0:T(4,128)(2,1)S(1)}, u32[]{:S(2)}, u32[]{:S(2)}) collective-permute-start(bf16[8,4,8192]{2,1,0:T(4,128)(2,1)S(1)} %constant_dynamic-update-slice_fusion.refs_0_), channel_id=1, source_target_pairs={{0,12},{2,50},{4,0},{6,54},{8,4},{10,58},{12,8},{14,62},{16,28},{1... | collective-permute-start | bytes 1572872 | tf_op jit(solution)/shard_map/ppermute | solution.py:29
  24.1 7.2 %collective-permute-done.5.refs_0_ = bf16[8,4,8192]{2,1,0:T(4,128)(2,1)S(1)} collective-permute-done((bf16[8,4,8192]{2,1,0:T(4,128)(2,1)S(1)}, bf16[8,4,8192]{2,1,0:T(4,128)(2,1)S(1)}, u32[]{:S(2)}, u32[]{:S(2)}) %collective-permute-start.5) | collective-permute-done | bytes 524320 | tf_op jit(solution)/shard_map/ppermute | solution.py:29
  31.8 2.1 %copy-done = bf16[231,8192]{1,0:T(8,128)(2,1)S(1)} copy-done((bf16[231,8192]{1,0:T(8,128)(2,1)S(1)}, bf16[231,8192]{1,0:T(8,128)(2,1)}, u32[]{:S(2)}) %copy-start) | copy-done | bytes 3784728
  33.9 2.1 %copy-done.3 = bf16[231,8192]{1,0:T(8,128)(2,1)S(1)} copy-done((bf16[231,8192]{1,0:T(8,128)(2,1)S(1)}, bf16[231,8192]{1,0:T(8,128)(2,1)}, u32[]{:S(2)}) %copy-start.3) | copy-done | bytes 3784728
  35.9 2.2 %shard_map.50.hidden_ref = bf16[64,231]{1,0:T(8,128)(2,1)S(1)} custom-call(bf16[8,4,8192]{2,1,0:T(4,128)(2,1)S(1)} %constant_dynamic-update-slice_fusion.refs_0_, bf16[8,4,8192]{2,1,0:T(4,128)(2,1)S(1)} %collective-permute-done.15.refs_1_, bf16[231,8192]{1,0:T(8,128)(2,1)S(1)} %copy-done, bf16[231,8192]{1,0:T(8,128)(2,1)S(1)} %copy-done.3), custom_call_target="tpu_custom_call" | custom-call | tf_op jit(solution)/shard_map/pallas_call | solution.py:138
  38.2 0.8 shard_map.51
  39.2 3.3 %collective-permute-start.8 = (bf16[4,4,8192]{2,1,0:T(4,128)(2,1)S(1)}, bf16[4,4,8192]{2,1,0:T(4,128)(2,1)S(1)}, u32[]{:S(2)}, u32[]{:S(2)}) collective-permute-start(bf16[4,4,8192]{2,1,0:T(4,128)(2,1)S(1)} %slice.9), channel_id=1, source_target_pairs={{0,12},{2,50},{4,0},{6,54},{8,4},{10,58},{12,8},{14,62},{16,28},{1... | collective-permute-start | bytes 786440 | tf_op jit(solution)/shard_map/ppermute | solution.py:29
  42.8 3.0 %shard_map.49 = (bf16[16,2,8192]{2,1,0:T(2,128)(2,1)S(1)}, bf16[16,2,8192]{2,1,0:T(2,128)(2,1)S(1)}, f32[64,8192]{1,0:T(8,128)S(1)}) custom-call(bf16[8,4,8192]{2,1,0:T(4,128)(2,1)S(1)} %collective-permute-done.5.refs_0_, bf16[8,4,8192]{2,1,0:T(4,128)(2,1)S(1)} %collective-permute-done.7.refs_1_, bf16[8,4,8192]{2,1,0:T(4,128)(2,1)S(1)} %collective-permute-done.12.refs_2_, ...), custom_call_target="tpu_custom_call" | custom-call | tf_op jit(solution)/shard_map/pallas_call | solution.py:138
  46.9 3.3 %collective-permute-done.6.refs_0_ = bf16[4,4,8192]{2,1,0:T(4,128)(2,1)S(1)} collective-permute-done((bf16[4,4,8192]{2,1,0:T(4,128)(2,1)S(1)}, bf16[4,4,8192]{2,1,0:T(4,128)(2,1)S(1)}, u32[]{:S(2)}, u32[]{:S(2)}) %collective-permute-start.6) | collective-permute-done | bytes 262176 | tf_op jit(solution)/shard_map/ppermute | solution.py:29
  51.0 1.6 %collective-permute-start.17 = (bf16[8,2,8192]{2,1,0:T(2,128)(2,1)S(1)}, bf16[8,2,8192]{2,1,0:T(2,128)(2,1)S(1)}, u32[]{:S(2)}, u32[]{:S(2)}) collective-permute-start(bf16[8,2,8192]{2,1,0:T(2,128)(2,1)S(1)} %get-tuple-element.20), channel_id=1, source_target_pairs={{0,4},{2,18},{4,8},{6,22},{8,12},{10,26},{12,0},{14,30},{16,20},{1... | collective-permute-start | bytes 786440 | tf_op jit(solution)/shard_map/ppermute | solution.py:29
  52.7 3.0 %shard_map.48 = (bf16[16,2,8192]{2,1,0:T(2,128)(2,1)S(1)}, f32[32,8192]{1,0:T(8,128)S(1)}) custom-call(bf16[4,4,8192]{2,1,0:T(4,128)(2,1)S(1)} %collective-permute-done.6.refs_0_, bf16[4,4,8192]{2,1,0:T(4,128)(2,1)S(1)} %collective-permute-done.8.refs_1_, bf16[4,4,8192]{2,1,0:T(4,128)(2,1)S(1)} %collective-permute-done.9.refs_2_, ...), custom_call_target="tpu_custom_call" | custom-call | tf_op jit(solution)/shard_map/pallas_call | solution.py:138
  55.8 1.2 %collective-permute-done.20.lent_ref = bf16[8,2,8192]{2,1,0:T(2,128)(2,1)S(1)} collective-permute-done((bf16[8,2,8192]{2,1,0:T(2,128)(2,1)S(1)}, bf16[8,2,8192]{2,1,0:T(2,128)(2,1)S(1)}, u32[]{:S(2)}, u32[]{:S(2)}) %collective-permute-start.20) | collective-permute-done | bytes 262176 | tf_op jit(solution)/shard_map/ppermute | solution.py:29
  57.3 1.7 %collective-permute-start.21 = (bf16[16,2,8192]{2,1,0:T(2,128)(2,1)S(1)}, bf16[16,2,8192]{2,1,0:T(2,128)(2,1)S(1)}, u32[]{:S(2)}, u32[]{:S(2)}) collective-permute-start(bf16[16,2,8192]{2,1,0:T(2,128)(2,1)S(1)} %shard_map.54), channel_id=1, source_target_pairs={{0,12},{2,50},{4,0},{6,54},{8,4},{10,58},{12,8},{14,62},{16,28},{1... | collective-permute-start | bytes 1572872 | tf_op jit(solution)/shard_map/ppermute | solution.py:29
  59.9 6.7 %collective-permute-done.21.high_ref = bf16[16,2,8192]{2,1,0:T(2,128)(2,1)S(1)} collective-permute-done((bf16[16,2,8192]{2,1,0:T(2,128)(2,1)S(1)}, bf16[16,2,8192]{2,1,0:T(2,128)(2,1)S(1)}, u32[]{:S(2)}, u32[]{:S(2)}) %collective-permute-start.21) | collective-permute-done | bytes 524320 | tf_op jit(solution)/shard_map/ppermute | solution.py:29
  66.6 3.2 %collective-permute-done.18.low_ref = bf16[16,2,8192]{2,1,0:T(2,128)(2,1)S(1)} collective-permute-done((bf16[16,2,8192]{2,1,0:T(2,128)(2,1)S(1)}, bf16[16,2,8192]{2,1,0:T(2,128)(2,1)S(1)}, u32[]{:S(2)}, u32[]{:S(2)}) %collective-permute-start.18) | collective-permute-done | bytes 524320 | tf_op jit(solution)/shard_map/ppermute | solution.py:29
  69.8 1.4 %shard_map.55 = bf16[16,2,8192]{2,1,0:T(2,128)(2,1)} custom-call(f32[32,8192]{1,0:T(8,128)S(1)} %get-tuple-element.14.own_ref, bf16[16,2,8192]{2,1,0:T(2,128)(2,1)S(1)} %collective-permute-done.11.fold_ref, bf16[16,2,8192]{2,1,0:T(2,128)(2,1)S(1)} %collective-permute-done.18.low_ref, bf16[16,2,8192]{2,1,0:T(2,128)(2,1)S(1)} %collective-permute-done.21.high_ref), custom_call_target="tpu_custom_call" | custom-call | tf_op jit(solution)/shard_map/pallas_call | solution.py:138
  71.2 5.9 %all-to-all-start = ((bf16[16,2,8192]{2,1,0:T(2,128)(2,1)}), bf16[16,2,8192]{2,1,0:T(2,128)(2,1)S(1)}, u32[]{:S(2)}, u32[]{:S(2)}) async-start(bf16[16,2,8192]{2,1,0:T(2,128)(2,1)} %shard_map.55), calls=%async_computation | async-start | bytes 1048576 | tf_op jit(solution)/shard_map/all_to_all | solution.py:239
  77.2 2.1 %copy-done.2 = bf16[231,8192]{1,0:T(8,128)(2,1)S(1)} copy-done((bf16[231,8192]{1,0:T(8,128)(2,1)S(1)}, bf16[231,8192]{1,0:T(8,128)(2,1)}, u32[]{:S(2)}) %copy-start.2) | copy-done | bytes 3784728
  79.2 0.6 shard_map.46
  79.8 1.5 %copy-done.5 = bf16[231,8192]{1,0:T(8,128)(2,1)S(1)} copy-done((bf16[231,8192]{1,0:T(8,128)(2,1)S(1)}, bf16[231,8192]{1,0:T(8,128)(2,1)}, u32[]{:S(2)}) %copy-start.5) | copy-done | bytes 3784728
  81.9 4.9 %all-to-all-done = bf16[16,2,8192]{2,1,0:T(2,128)(2,1)S(1)} async-done(((bf16[16,2,8192]{2,1,0:T(2,128)(2,1)}), bf16[16,2,8192]{2,1,0:T(2,128)(2,1)S(1)}, u32[]{:S(2)}, u32[]{:S(2)}) %all-to-all-start) | async-done | bytes 524320 | tf_op jit(solution)/shard_map/all_to_all | solution.py:239
  86.8 1.1 %reduce_sum.12 = bf16[2,8192]{1,0:T(2,128)(2,1)} reduce(bf16[16,2,8192]{2,1,0:T(2,128)(2,1)S(1)} %all-to-all-done, bf16[]{:T(256)} %constant.2.clone.1), dimensions={0}, to_apply=%region_0.0 | reduce | flops 245760 | bytes 557058 | tf_op jit(solution)/shard_map/reduce_sum | solution.py:242
  (47 shorter events, 5.3 us)
Async XLA Ops:
  0.0 6.4 %collective-permute-start = (bf16[4,8192]{1,0:T(4,128)(2,1)}, bf16[4,8192]{1,0:T(4,128)(2,1)S(1)}, u32[]{:S(2)}, u32[]{:S(2)}) collective-permute-start(bf16[4,8192]{1,0:T(4,128)(2,1)} %param.4), channel_id=1, source_target_pairs={{0,8},{2,34},{4,12},{6,38},{8,0},{10,42},{12,4},{14,46},{16,24},{1... | collective-permute-start | bytes 196616 | tf_op jit(solution)/shard_map/ppermute | solution.py:29
  4.0 6.9 %collective-permute-start.1 = (bf16[4,8192]{1,0:T(4,128)(2,1)}, bf16[4,8192]{1,0:T(4,128)(2,1)S(1)}, u32[]{:S(2)}, u32[]{:S(2)}) collective-permute-start(bf16[4,8192]{1,0:T(4,128)(2,1)} %param.4), channel_id=1, source_target_pairs={{0,72},{2,98},{4,76},{6,102},{8,64},{10,106},{12,68},{14,110},{16,... | collective-permute-start | bytes 196616 | tf_op jit(solution)/shard_map/ppermute | solution.py:29
  11.0 6.2 %collective-permute-start.2 = (bf16[2,4,8192]{2,1,0:T(4,128)(2,1)S(1)}, bf16[2,4,8192]{2,1,0:T(4,128)(2,1)S(1)}, u32[]{:S(2)}, u32[]{:S(2)}) collective-permute-start(bf16[2,4,8192]{2,1,0:T(4,128)(2,1)S(1)} %pad_maximum_fusion), channel_id=1, source_target_pairs={{0,16},{2,6},{4,20},{6,10},{8,24},{10,14},{12,28},{14,2},{16,32},{... | collective-permute-start | bytes 393224 | tf_op jit(solution)/shard_map/ppermute | solution.py:29
  12.6 5.0 %collective-permute-start.3 = (bf16[2,4,8192]{2,1,0:T(4,128)(2,1)S(1)}, bf16[2,4,8192]{2,1,0:T(4,128)(2,1)S(1)}, u32[]{:S(2)}, u32[]{:S(2)}) collective-permute-start(bf16[2,4,8192]{2,1,0:T(4,128)(2,1)S(1)} %pad_maximum_fusion), channel_id=1, source_target_pairs={{0,48},{2,14},{4,52},{6,2},{8,56},{10,6},{12,60},{14,10},{16,0},{1... | collective-permute-start | bytes 393224 | tf_op jit(solution)/shard_map/ppermute | solution.py:29
  14.3 6.5 %collective-permute-start.4 = (bf16[2,4,8192]{2,1,0:T(4,128)(2,1)S(1)}, bf16[2,4,8192]{2,1,0:T(4,128)(2,1)S(1)}, u32[]{:S(2)}, u32[]{:S(2)}) collective-permute-start(bf16[2,4,8192]{2,1,0:T(4,128)(2,1)S(1)} %pad_maximum_fusion), channel_id=1, source_target_pairs={{0,32},{2,10},{4,36},{6,14},{8,40},{10,2},{12,44},{14,6},{16,48},{... | collective-permute-start | bytes 393224 | tf_op jit(solution)/shard_map/ppermute | solution.py:29
  20.8 10.5 %collective-permute-start.5 = (bf16[8,4,8192]{2,1,0:T(4,128)(2,1)S(1)}, bf16[8,4,8192]{2,1,0:T(4,128)(2,1)S(1)}, u32[]{:S(2)}, u32[]{:S(2)}) collective-permute-start(bf16[8,4,8192]{2,1,0:T(4,128)(2,1)S(1)} %constant_dynamic-update-slice_fusion.refs_0_), channel_id=1, source_target_pairs={{0,4},{2,18},{4,8},{6,22},{8,12},{10,26},{12,0},{14,30},{16,20},{1... | collective-permute-start | bytes 1572872 | tf_op jit(solution)/shard_map/ppermute | solution.py:29
  21.9 9.4 %collective-permute-start.7 = (bf16[8,4,8192]{2,1,0:T(4,128)(2,1)S(1)}, bf16[8,4,8192]{2,1,0:T(4,128)(2,1)S(1)}, u32[]{:S(2)}, u32[]{:S(2)}) collective-permute-start(bf16[8,4,8192]{2,1,0:T(4,128)(2,1)S(1)} %constant_dynamic-update-slice_fusion.refs_0_), channel_id=1, source_target_pairs={{0,12},{2,50},{4,0},{6,54},{8,4},{10,58},{12,8},{14,62},{16,28},{1... | collective-permute-start | bytes 1572872 | tf_op jit(solution)/shard_map/ppermute | solution.py:29
  24.1 7.7 %collective-permute-start.15 = (bf16[8,4,8192]{2,1,0:T(4,128)(2,1)S(1)}, bf16[8,4,8192]{2,1,0:T(4,128)(2,1)S(1)}, u32[]{:S(2)}, u32[]{:S(2)}) collective-permute-start(bf16[8,4,8192]{2,1,0:T(4,128)(2,1)S(1)} %constant_dynamic-update-slice_fusion.refs_0_), channel_id=1, source_target_pairs={{0,2},{2,0},{4,6},{6,4},{8,10},{10,8},{12,14},{14,12},{16,18},{18,... | collective-permute-start | bytes 1572872 | tf_op jit(solution)/shard_map/ppermute | solution.py:29
  31.3 11.4 %collective-permute-start.12 = (bf16[8,4,8192]{2,1,0:T(4,128)(2,1)S(1)}, bf16[8,4,8192]{2,1,0:T(4,128)(2,1)S(1)}, u32[]{:S(2)}, u32[]{:S(2)}) collective-permute-start(bf16[8,4,8192]{2,1,0:T(4,128)(2,1)S(1)} %collective-permute-done.5.refs_0_), channel_id=1, source_target_pairs={{0,2},{2,0},{4,6},{6,4},{8,10},{10,8},{12,14},{14,12},{16,18},{18,... | collective-permute-start | bytes 1572872 | tf_op jit(solution)/shard_map/ppermute | solution.py:29
  31.3 11.4 %collective-permute-start.13 = (bf16[8,4,8192]{2,1,0:T(4,128)(2,1)S(1)}, bf16[8,4,8192]{2,1,0:T(4,128)(2,1)S(1)}, u32[]{:S(2)}, u32[]{:S(2)}) collective-permute-start(bf16[8,4,8192]{2,1,0:T(4,128)(2,1)S(1)} %collective-permute-done.7.refs_1_), channel_id=1, source_target_pairs={{0,2},{2,0},{4,6},{6,4},{8,10},{10,8},{12,14},{14,12},{16,18},{18,... | collective-permute-start | bytes 1572872 | tf_op jit(solution)/shard_map/ppermute | solution.py:29
  31.8 2.1 %copy-start = (bf16[231,8192]{1,0:T(8,128)(2,1)S(1)}, bf16[231,8192]{1,0:T(8,128)(2,1)}, u32[]{:S(2)}) copy-start(bf16[231,8192]{1,0:T(8,128)(2,1)} %refs_2_.1) | copy-start | bytes 11354116
  33.9 2.1 %copy-start.3 = (bf16[231,8192]{1,0:T(8,128)(2,1)S(1)}, bf16[231,8192]{1,0:T(8,128)(2,1)}, u32[]{:S(2)}) copy-start(bf16[231,8192]{1,0:T(8,128)(2,1)} %refs_3_.1) | copy-start | bytes 11354116
  35.9 2.3 %copy-start.6 = (bf16[231,8192]{1,0:T(8,128)(2,1)S(1)}, bf16[231,8192]{1,0:T(8,128)(2,1)}, u32[]{:S(2)}) copy-start(bf16[231,8192]{1,0:T(8,128)(2,1)} %refs_0_.5) | copy-start | bytes 11354116
  35.9 6.8 %copy-start.4 = (bf16[231,8192]{1,0:T(8,128)(2,1)S(1)}, bf16[231,8192]{1,0:T(8,128)(2,1)}, u32[]{:S(2)}) copy-start(bf16[231,8192]{1,0:T(8,128)(2,1)} %refs_3_.1) | copy-start | bytes 11354116
  38.2 4.5 %copy-start.1 = (bf16[231,8192]{1,0:T(8,128)(2,1)S(1)}, bf16[231,8192]{1,0:T(8,128)(2,1)}, u32[]{:S(2)}) copy-start(bf16[231,8192]{1,0:T(8,128)(2,1)} %refs_2_.1) | copy-start | bytes 11354116
  39.0 11.2 %collective-permute-start.16 = (bf16[16,2,8192]{2,1,0:T(2,128)(2,1)S(1)}, bf16[16,2,8192]{2,1,0:T(2,128)(2,1)S(1)}, u32[]{:S(2)}, u32[]{:S(2)}) collective-permute-start(bf16[16,2,8192]{2,1,0:T(2,128)(2,1)S(1)} %get-tuple-element.19), channel_id=1, source_target_pairs={{0,2},{2,0},{4,6},{6,4},{8,10},{10,8},{12,14},{14,12},{16,18},{18,... | collective-permute-start | bytes 1572872 | tf_op jit(solution)/shard_map/ppermute | solution.py:29
  39.2 7.2 %collective-permute-start.8 = (bf16[4,4,8192]{2,1,0:T(4,128)(2,1)S(1)}, bf16[4,4,8192]{2,1,0:T(4,128)(2,1)S(1)}, u32[]{:S(2)}, u32[]{:S(2)}) collective-permute-start(bf16[4,4,8192]{2,1,0:T(4,128)(2,1)S(1)} %slice.9), channel_id=1, source_target_pairs={{0,12},{2,50},{4,0},{6,54},{8,4},{10,58},{12,8},{14,62},{16,28},{1... | collective-permute-start | bytes 786440 | tf_op jit(solution)/shard_map/ppermute | solution.py:29
  42.6 7.7 %collective-permute-start.6 = (bf16[4,4,8192]{2,1,0:T(4,128)(2,1)S(1)}, bf16[4,4,8192]{2,1,0:T(4,128)(2,1)S(1)}, u32[]{:S(2)}, u32[]{:S(2)}) collective-permute-start(bf16[4,4,8192]{2,1,0:T(4,128)(2,1)S(1)} %slice.8), channel_id=1, source_target_pairs={{0,4},{2,18},{4,8},{6,22},{8,12},{10,26},{12,0},{14,30},{16,20},{1... | collective-permute-start | bytes 786440 | tf_op jit(solution)/shard_map/ppermute | solution.py:29
  45.8 11.2 %collective-permute-start.19 = (bf16[16,2,8192]{2,1,0:T(2,128)(2,1)S(1)}, bf16[16,2,8192]{2,1,0:T(2,128)(2,1)S(1)}, u32[]{:S(2)}, u32[]{:S(2)}) collective-permute-start(bf16[16,2,8192]{2,1,0:T(2,128)(2,1)S(1)} %get-tuple-element.21), channel_id=1, source_target_pairs={{0,2},{2,0},{4,6},{6,4},{8,10},{10,8},{12,14},{14,12},{16,18},{18,... | collective-permute-start | bytes 1572872 | tf_op jit(solution)/shard_map/ppermute | solution.py:29
  46.4 4.6 %collective-permute-start.10 = (bf16[4,4,8192]{2,1,0:T(4,128)(2,1)S(1)}, bf16[4,4,8192]{2,1,0:T(4,128)(2,1)S(1)}, u32[]{:S(2)}, u32[]{:S(2)}) collective-permute-start(bf16[4,4,8192]{2,1,0:T(4,128)(2,1)S(1)} %collective-permute-done.8.refs_1_), channel_id=1, source_target_pairs={{0,2},{2,0},{4,6},{6,4},{8,10},{10,8},{12,14},{14,12},{16,18},{18,... | collective-permute-start | bytes 786440 | tf_op jit(solution)/shard_map/ppermute | solution.py:29
  46.4 12.6 %collective-permute-start.14 = (bf16[16,2,8192]{2,1,0:T(2,128)(2,1)S(1)}, bf16[16,2,8192]{2,1,0:T(2,128)(2,1)S(1)}, u32[]{:S(2)}, u32[]{:S(2)}) collective-permute-start(bf16[16,2,8192]{2,1,0:T(2,128)(2,1)S(1)} %get-tuple-element.17), channel_id=1, source_target_pairs={{0,2},{2,0},{4,6},{6,4},{8,10},{10,8},{12,14},{14,12},{16,18},{18,... | collective-permute-start | bytes 1572872 | tf_op jit(solution)/shard_map/ppermute | solution.py:29
  50.3 2.4 %collective-permute-start.9 = (bf16[4,4,8192]{2,1,0:T(4,128)(2,1)S(1)}, bf16[4,4,8192]{2,1,0:T(4,128)(2,1)S(1)}, u32[]{:S(2)}, u32[]{:S(2)}) collective-permute-start(bf16[4,4,8192]{2,1,0:T(4,128)(2,1)S(1)} %collective-permute-done.6.refs_0_), channel_id=1, source_target_pairs={{0,2},{2,0},{4,6},{6,4},{8,10},{10,8},{12,14},{14,12},{16,18},{18,... | collective-permute-start | bytes 786440 | tf_op jit(solution)/shard_map/ppermute | solution.py:29
  50.6 6.4 %collective-permute-start.20 = (bf16[8,2,8192]{2,1,0:T(2,128)(2,1)S(1)}, bf16[8,2,8192]{2,1,0:T(2,128)(2,1)S(1)}, u32[]{:S(2)}, u32[]{:S(2)}) collective-permute-start(bf16[8,2,8192]{2,1,0:T(2,128)(2,1)S(1)} %get-tuple-element.22), channel_id=1, source_target_pairs={{0,12},{2,50},{4,0},{6,54},{8,4},{10,58},{12,8},{14,62},{16,28},{1... | collective-permute-start | bytes 786440 | tf_op jit(solution)/shard_map/ppermute | solution.py:29
  51.0 8.0 %collective-permute-start.17 = (bf16[8,2,8192]{2,1,0:T(2,128)(2,1)S(1)}, bf16[8,2,8192]{2,1,0:T(2,128)(2,1)S(1)}, u32[]{:S(2)}, u32[]{:S(2)}) collective-permute-start(bf16[8,2,8192]{2,1,0:T(2,128)(2,1)S(1)} %get-tuple-element.20), channel_id=1, source_target_pairs={{0,4},{2,18},{4,8},{6,22},{8,12},{10,26},{12,0},{14,30},{16,20},{1... | collective-permute-start | bytes 786440 | tf_op jit(solution)/shard_map/ppermute | solution.py:29
  55.7 4.2 %collective-permute-start.11 = (bf16[16,2,8192]{2,1,0:T(2,128)(2,1)S(1)}, bf16[16,2,8192]{2,1,0:T(2,128)(2,1)S(1)}, u32[]{:S(2)}, u32[]{:S(2)}) collective-permute-start(bf16[16,2,8192]{2,1,0:T(2,128)(2,1)S(1)} %get-tuple-element.15), channel_id=1, source_target_pairs={{0,2},{2,0},{4,6},{6,4},{8,10},{10,8},{12,14},{14,12},{16,18},{18,... | collective-permute-start | bytes 1572872 | tf_op jit(solution)/shard_map/ppermute | solution.py:29
  57.3 9.3 %collective-permute-start.21 = (bf16[16,2,8192]{2,1,0:T(2,128)(2,1)S(1)}, bf16[16,2,8192]{2,1,0:T(2,128)(2,1)S(1)}, u32[]{:S(2)}, u32[]{:S(2)}) collective-permute-start(bf16[16,2,8192]{2,1,0:T(2,128)(2,1)S(1)} %shard_map.54), channel_id=1, source_target_pairs={{0,12},{2,50},{4,0},{6,54},{8,4},{10,58},{12,8},{14,62},{16,28},{1... | collective-permute-start | bytes 1572872 | tf_op jit(solution)/shard_map/ppermute | solution.py:29
  59.4 10.5 %collective-permute-start.18 = (bf16[16,2,8192]{2,1,0:T(2,128)(2,1)S(1)}, bf16[16,2,8192]{2,1,0:T(2,128)(2,1)S(1)}, u32[]{:S(2)}, u32[]{:S(2)}) collective-permute-start(bf16[16,2,8192]{2,1,0:T(2,128)(2,1)S(1)} %shard_map.53), channel_id=1, source_target_pairs={{0,4},{2,18},{4,8},{6,22},{8,12},{10,26},{12,0},{14,30},{16,20},{1... | collective-permute-start | bytes 1572872 | tf_op jit(solution)/shard_map/ppermute | solution.py:29
  71.2 15.6 %all-to-all-start = ((bf16[16,2,8192]{2,1,0:T(2,128)(2,1)}), bf16[16,2,8192]{2,1,0:T(2,128)(2,1)S(1)}, u32[]{:S(2)}, u32[]{:S(2)}) async-start(bf16[16,2,8192]{2,1,0:T(2,128)(2,1)} %shard_map.55), calls=%async_computation | async-start | bytes 1048576 | tf_op jit(solution)/shard_map/all_to_all | solution.py:239
  77.1 2.1 %copy-start.2 = (bf16[231,8192]{1,0:T(8,128)(2,1)S(1)}, bf16[231,8192]{1,0:T(8,128)(2,1)}, u32[]{:S(2)}) copy-start(bf16[231,8192]{1,0:T(8,128)(2,1)} %refs_2_.1) | copy-start | bytes 11354116
  79.2 2.1 %copy-start.5 = (bf16[231,8192]{1,0:T(8,128)(2,1)S(1)}, bf16[231,8192]{1,0:T(8,128)(2,1)}, u32[]{:S(2)}) copy-start(bf16[231,8192]{1,0:T(8,128)(2,1)} %refs_3_.1) | copy-start | bytes 11354116
